TPU v7x, 32 devices: a whole 2x2x4 slice. The times are simulated.
32 devices in a mesh: member: 8 (over z, y), region: 4 (over x, core).
Axes of the slice: x: 2, y: 2, z: 4, core: 2. Of those that a mesh axis runs over, the one named last changes fastest.
Arguments:
- ensemble: bfloat16 [512, 32768], P(('member', 'region')), may hold values from -12 to 12
- obs_offset: int32 [4, 8, 16], P('region', 'member'), may hold values from 0 to 1023
- observed: float32 [4, 8, 16], P('region', 'member'), may hold values from -12 to 12
- obs_var: float32 [4, 8, 16], P('region', 'member'), may hold values from 0.2 to 2
Outputs:
- analysis: bfloat16 [512, 32768], P(('member', 'region'))
Inputs may be any that keep to these rules, and one draw needn't show every extreme that they name: obs_offset indexes a link within the block of 1024 links; two detectors may watch the same link.
All inputs are finite; a program needn't handle non-finite values.
Results may differ from a plain program's by a relative error of at most 0.0019.
Values may be sent and summed in bfloat16 or wider, within the bound.
A program may use at most 128 MiB of HBM per device.

v0:
```python
import jax
import jax.numpy as jnp
from jax import lax
from jax.sharding import PartitionSpec as P


def observation_terms(picked, values, variance, ensemble_size):
    center = jnp.mean(picked, axis=1, keepdims=True)
    anomaly = picked - center
    innovation = values - center[:, 0]
    numer = jnp.sum(innovation * innovation)
    denom = jnp.sum(jnp.sum(anomaly * anomaly, axis=1) / (ensemble_size - 1.0) + variance)
    weight = 1.0 / ((ensemble_size - 1.0) * variance)
    return (anomaly, innovation, weight, numer, denom)


def weighted_products(anomaly, innovation, weight):
    weighted = anomaly * weight[:, None]
    products = jnp.dot(weighted.T, anomaly, precision=lax.Precision.HIGHEST)
    column = jnp.dot(innovation * weight, anomaly, precision=lax.Precision.HIGHEST)
    return (products, column)


def mixing_matrix(products, column, lift, diag_coef, col_coef, mat_coef):
    identity = jnp.eye(products.shape[0], dtype=jnp.float32)
    system = identity + lift * products
    factor = jnp.linalg.cholesky(system)
    right_side = jnp.concatenate([products, column[:, None]], axis=1)
    solved = jax.scipy.linalg.cho_solve((factor, True), right_side)
    return diag_coef * identity + col_coef * solved[:, -1][None, :] - mat_coef * solved[:, :-1]


def local(ensemble, obs_offset, observed, obs_var):
    members = lax.axis_size("member")
    regions = lax.axis_size("region")
    own_count = ensemble.shape[0]
    ensemble_size = own_count * members * regions
    link_count = ensemble.shape[1] // (members * regions)
    shifted = lax.all_to_all(
        lax.all_to_all(ensemble, "region", split_axis=1, concat_axis=0, tiled=True),
        "member",
        split_axis=1,
        concat_axis=0,
        tiled=True,
    )
    values = observed.reshape(-1)
    variance = obs_var.reshape(-1)
    region_offsets = lax.all_gather(obs_offset, "member", axis=1, tiled=True)
    every_offset = lax.all_gather(region_offsets, "region", axis=0, tiled=True)
    region_block = lax.broadcasted_iota(jnp.int32, every_offset.shape, 0)
    member_block = lax.broadcasted_iota(jnp.int32, every_offset.shape, 1)
    link_index = ((region_block * members + member_block) * link_count + every_offset).reshape(-1)
    own_rows = jnp.take(ensemble, link_index, axis=1).reshape(own_count, regions, -1)
    local_rows = lax.all_to_all(own_rows, "region", split_axis=1, concat_axis=0, tiled=True)
    local_rows = local_rows.reshape(own_count * regions, -1)
    obs_rows = lax.all_gather(local_rows, "member", axis=0, tiled=True)
    region_values, region_variance = (
        lax.all_gather(values, "member", axis=0, tiled=True),
        lax.all_gather(variance, "member", axis=0, tiled=True),
    )
    picked = obs_rows.T.astype(jnp.float32)
    anomaly, innovation, weight, numer, denom = observation_terms(
        picked, region_values, region_variance, ensemble_size
    )
    numer, denom = lax.psum((numer, denom), "region")
    inflation = jnp.sqrt(numer / denom)
    products, column = weighted_products(inflation * anomaly, innovation, weight)
    products, column = lax.psum((products, column), "region")
    mixing = mixing_matrix(products, column, 1.0, inflation, inflation, 0.5 * inflation)
    state_values = shifted.astype(jnp.float32)
    center = jnp.mean(state_values, axis=0, keepdims=True)
    updated = (
        center + jnp.dot(mixing, state_values - center, precision=lax.Precision.HIGHEST)
    ).astype(jnp.bfloat16)
    return lax.all_to_all(
        lax.all_to_all(updated, "member", split_axis=0, concat_axis=1, tiled=True),
        "region",
        split_axis=0,
        concat_axis=1,
        tiled=True,
    )


def solution(mesh):
    return jax.shard_map(
        local,
        mesh=mesh,
        in_specs=(
            P(("member", "region"), None),
            P("region", "member", None),
            P("region", "member", None),
            P("region", "member", None),
        ),
        out_specs=P(("member", "region"), None),
        check_vma=False,
    )
```

profile of v0, /device:TPU:0, one launch (start us, length us, event | category | flops | bytes accessed | tf_op | source)
XLA Modules:
  0.0 394.1 jit_solution(4288350001859366908)
XLA Ops:
  6.5 22.5 %all_gather.16 = s32[1,8,16]{2,0,1:T(1,128)S(1)} all-gather(s32[1,1,16]{2,0,1:T(1,128)} %bitcast.112), channel_id=1, replica_groups=mesh['member'=8,'region'=4] {'member'}, dimensions={1}, use_global_device_ids=true | all-gather | bytes 576 | tf_op jit(solution)/shard_map/all_gather | solution.py:48
  29.0 5.2 %all_gather.17 = s32[4,8,16]{2,1,0:T(8,128)S(1)} all-gather(s32[1,8,16]{2,1,0:T(8,128)S(1)} %bitcast.109), channel_id=1, replica_groups=mesh['member'=8,'region'=4] {'region'}, dimensions={0}, use_global_device_ids=true | all-gather | bytes 2560 | tf_op jit(solution)/shard_map/all_gather | solution.py:49
  34.5 7.1 %copy.51 = bf16[16,32768]{0,1:T(8,128)(2,1)} copy(bf16[16,32768]{1,0:T(8,128)(2,1)} %param.4) | data formatting | bytes 2097152 | tf_op args[0]
  41.5 5.6 %gather_fusion = bf16[512,16]{1,0:T(8,128)(2,1)S(1)} fusion(bf16[16,32768]{0,1:T(8,128)(2,1)} %copy.51, s32[1024]{0:T(1024)S(1)} %pad_clamp_fusion), kind=kCustom, calls=%fused_computation | custom fusion | bytes 34816 | tf_op jit(solution)/shard_map/jit(_take)/gather | solution.py:53
  52.8 17.1 %all-reduce.3 = (f32[128]{0:T(128)S(1)}, f32[128]{0:T(128)S(1)}) all-reduce(f32[128]{0:T(128)S(1)} %bitcast_dynamic-update-slice_fusion.1, f32[128]{0:T(128)S(1)} %bitcast_dynamic-update-slice_fusion.2), channel_id=3, replica_groups=mesh['member'=8,'region'=4] {'member'}, use_global_device_ids=true, to_apply=%add.2 | all-reduce | flops 256 | bytes 2048 | tf_op jit(solution)/shard_map/all_gather | solution.py:59
  69.9 30.5 %all_gather.18 = bf16[512,128]{1,0:T(8,128)(2,1)S(1)} all-gather(bf16[64,128]{1,0:T(8,128)(2,1)S(1)} %bitcast.108), channel_id=1, replica_groups=mesh['member'=8,'region'=4] {'member'}, dimensions={0}, use_global_device_ids=true | all-gather | bytes 147456 | tf_op jit(solution)/shard_map/all_gather | solution.py:56
  101.8 6.3 %all-reduce.4 = (f32[]{:T(128)}, f32[]{:T(128)}) all-reduce(f32[]{:T(128)} %get-tuple-element.54, f32[]{:T(128)} %get-tuple-element.51), channel_id=1, replica_groups=mesh['member'=8,'region'=4] {'region'}, use_global_device_ids=true, to_apply=%region_3.4 | all-reduce | flops 2 | bytes 16 | tf_op jit(solution)/shard_map/psum | solution.py:65
  112.5 4.2 %all-to-all-start = ((bf16[16,4,8192]{2,0,1:T(8,128)(2,1)}), bf16[16,4,8192]{2,0,1:T(8,128)(2,1)}, u32[]{:S(2)}, u32[]{:S(2)}) async-start(bf16[16,4,8192]{2,0,1:T(8,128)(2,1)} %bitcast.95), calls=%async_computation | async-start | bytes 2097152 | tf_op jit(solution)/shard_map/all_to_all | solution.py:40
  117.1 22.4 %psum.31 = f32[512,1]{0,1:T(1,128)S(1)} all-reduce(f32[512,1]{0,1:T(1,128)S(1)} %convolution_bitcast_fusion), channel_id=1, replica_groups=mesh['member'=8,'region'=4] {'region'}, use_global_device_ids=true, to_apply=%region_16.17 | all-reduce | flops 512 | bytes 4096 | tf_op jit(solution)/shard_map/psum | solution.py:68
  139.5 14.7 %all-reduce.7.cloned.1.call-done = f32[512,512]{0,1:T(8,128)} async-done(((f32[512,512]{0,1:T(8,128)}), f32[512,512]{0,1:T(8,128)}) %all-reduce.7.cloned.1.call-update) | async-done | bytes 1048592 | tf_op jit(solution)/shard_map/psum | solution.py:68
  158.7 11.7 %cholesky.103 = f32[128,128]{1,0:T(8,128)S(1)} custom-call(f32[128,128]{1,0:T(8,128)S(1)} %cholesky.263), custom_call_target="Cholesky" | custom-call | tf_op jit(solution)/shard_map/jit(cholesky)/cholesky | solution.py:27
  170.4 9.8 %custom-call.34 = f32[1,128,128]{1,2,0:T(8,128)S(1)} custom-call(f32[1,128,128]{2,1,0:T(8,128)S(1)} %get-tuple-element.50), custom_call_target="InvertDiagBlocksLowerTriangular" | custom-call | tf_op jit(solution)/shard_map/jit(cholesky)/cholesky | solution.py:27
  180.9 11.7 %cholesky.215 = f32[128,128]{1,0:T(8,128)S(1)} custom-call(f32[128,128]{1,0:T(8,128)S(1)} %cholesky.267), custom_call_target="Cholesky" | custom-call | tf_op jit(solution)/shard_map/jit(cholesky)/cholesky | solution.py:27
  193.0 10.0 %custom-call.35 = f32[1,128,128]{1,2,0:T(8,128)S(1)} custom-call(f32[1,128,128]{2,1,0:T(8,128)S(1)} %get-tuple-element.48), custom_call_target="InvertDiagBlocksLowerTriangular" | custom-call | tf_op jit(solution)/shard_map/jit(cholesky)/cholesky | solution.py:27
  205.0 11.7 %cholesky.236 = f32[128,128]{1,0:T(8,128)S(1)} custom-call(f32[128,128]{1,0:T(8,128)S(1)} %cholesky.272), custom_call_target="Cholesky" | custom-call | tf_op jit(solution)/shard_map/jit(cholesky)/cholesky | solution.py:27
  216.8 9.8 %custom-call.36 = f32[1,128,128]{1,2,0:T(8,128)S(1)} custom-call(f32[1,128,128]{2,1,0:T(8,128)S(1)} %get-tuple-element.46), custom_call_target="InvertDiagBlocksLowerTriangular" | custom-call | tf_op jit(solution)/shard_map/jit(cholesky)/cholesky | solution.py:27
  228.3 12.1 %cholesky.253 = f32[128,128]{1,0:T(8,128)S(1)} custom-call(f32[128,128]{1,0:T(8,128)S(1)} %convolution_subtract_fusion.8), custom_call_target="Cholesky" | custom-call | tf_op jit(solution)/shard_map/jit(cholesky)/cholesky | solution.py:27
  245.2 11.0 %while.1 = (s32[]{:T(128)}, f32[512,512]{0,1:T(8,128)S(1)}, s32[4,2]{0,1:T(2,128)S(1)}, f32[4,128,128]{2,1,0:T(8,128)}, s32[]{:T(128)}) while((s32[]{:T(128)}, f32[512,512]{0,1:T(8,128)S(1)}, s32[4,2]{0,1:T(2,128)S(1)}, f32[4,128,128]{2,1,0:T(8,128)}, s32[]{:T(128)}) %tuple.30), condition=%wide.while_cond, body=%wide.while_body.sunk | while | flops 2 | bytes 393829 | solution.py:29
  256.2 40.1 %custom-call.37 = f32[4,128,128]{1,2,0:T(8,128)S(1)} custom-call(f32[4,128,128]{2,1,0:T(8,128)} %get-tuple-element.12), custom_call_target="InvertDiagBlocksLowerTriangular" | custom-call | tf_op jit(solution)/shard_map/jit(_cho_solve)/triangular_solve | solution.py:29
  303.7 5.7 %all-to-all-start.1 = ((bf16[64,8,1024]{2,0,1:T(8,128)(2,1)}), bf16[64,8,1024]{2,0,1:T(8,128)(2,1)S(1)}, u32[]{:S(2)}, u32[]{:S(2)}) async-start(bf16[64,8,1024]{2,0,1:T(8,128)(2,1)} %copy.48), calls=%async_computation.1 | async-start | bytes 2097152 | tf_op jit(solution)/shard_map/all_to_all | solution.py:39
  314.6 20.2 %all-to-all-done.1 = bf16[64,8,1024]{2,0,1:T(8,128)(2,1)S(1)} async-done(((bf16[64,8,1024]{2,0,1:T(8,128)(2,1)}), bf16[64,8,1024]{2,0,1:T(8,128)(2,1)S(1)}, u32[]{:S(2)}, u32[]{:S(2)}) %all-to-all-start.1) | async-done | bytes 1048608 | tf_op jit(solution)/shard_map/all_to_all | solution.py:39
  335.3 3.7 add_convert_fusion
  338.9 29.1 %all_to_all.79 = bf16[8,64,1024]{2,1,0:T(8,128)(2,1)S(1)} all-to-all(bf16[8,64,1024]{2,1,0:T(8,128)(2,1)S(1)} %bitcast.106), channel_id=1, replica_groups=mesh['member'=8,'region'=4] {'member'}, dimensions={0} | all-to-all | bytes 2097152 | tf_op jit(solution)/shard_map/all_to_all | solution.py:76
  369.1 16.9 %all_to_all.80 = bf16[4,16,8192]{2,1,0:T(8,128)(2,1)S(1)} all-to-all(bf16[4,16,8192]{2,1,0:T(8,128)(2,1)S(1)} %all_to_all.70), channel_id=1, replica_groups=mesh['member'=8,'region'=4] {'region'}, dimensions={0} | all-to-all | bytes 2097152 | tf_op jit(solution)/shard_map/all_to_all | solution.py:75
  (115 shorter events, 47.4 us)
Async XLA Ops:
  34.4 16.7 %copy-start.5 = (u32[32]{0:T(128)S(1)}, u32[32]{0:T(128)}, u32[]{:S(2)}) copy-start(u32[32]{0:T(128)} %constant.210) | copy-start | bytes 388
  34.5 18.1 %copy-start.3 = (f32[1,1,16]{2,1,0:T(1,128)S(1)}, f32[1,1,16]{2,1,0:T(1,128)}, u32[]{:S(2)}) copy-start(f32[1,1,16]{2,1,0:T(1,128)} %param.7) | copy-start | bytes 196
  34.5 18.2 %copy-start.4 = (f32[1,1,16]{2,1,0:T(1,128)S(1)}, f32[1,1,16]{2,1,0:T(1,128)}, u32[]{:S(2)}) copy-start(f32[1,1,16]{2,1,0:T(1,128)} %param.6) | copy-start | bytes 196
  41.5 69.9 %copy-start.1 = (bf16[16,32768]{1,0:T(8,128)(2,1)S(1)}, bf16[16,32768]{1,0:T(8,128)(2,1)}, u32[]{:S(2)}) copy-start(bf16[16,32768]{1,0:T(8,128)(2,1)} %param.4) | copy-start | bytes 3145732
  47.9 22.0 %all-to-all-start.2 = ((bf16[16,4,128]{2,0,1:T(8,128)(2,1)}), bf16[16,4,128]{2,0,1:T(8,128)(2,1)S(1)}, u32[]{:S(2)}, u32[]{:S(2)}) async-start(bf16[16,4,128]{2,0,1:T(8,128)(2,1)} %broadcast_select_fusion), calls=%async_computation.2 | async-start | bytes 32768 | tf_op jit(solution)/shard_map/all_to_all | solution.py:54
  51.1 103.1 %all-reduce.7.cloned.1.call-start = ((), (), s32[]{:S(2)}) async-start(), calls=%async_computation.5 | async-start | bytes 2097152 | tf_op jit(solution)/shard_map/psum | solution.py:68
  112.5 187.8 %all-to-all-start = ((bf16[16,4,8192]{2,0,1:T(8,128)(2,1)}), bf16[16,4,8192]{2,0,1:T(8,128)(2,1)}, u32[]{:S(2)}, u32[]{:S(2)}) async-start(bf16[16,4,8192]{2,0,1:T(8,128)(2,1)} %bitcast.95), calls=%async_computation | async-start | bytes 2097152 | tf_op jit(solution)/shard_map/all_to_all | solution.py:40
  154.2 2.9 copy-start
  158.6 34.3 %copy-start.2 = (f32[512,512]{1,0:T(8,128)}, f32[512,512]{1,0:T(8,128)S(1)}, u32[]{:S(2)}) copy-start(f32[512,512]{1,0:T(8,128)S(1)} %fusion.4) | copy-start | bytes 3145732
  303.7 31.1 %all-to-all-start.1 = ((bf16[64,8,1024]{2,0,1:T(8,128)(2,1)}), bf16[64,8,1024]{2,0,1:T(8,128)(2,1)S(1)}, u32[]{:S(2)}, u32[]{:S(2)}) async-start(bf16[64,8,1024]{2,0,1:T(8,128)(2,1)} %copy.48), calls=%async_computation.1 | async-start | bytes 2097152 | tf_op jit(solution)/shard_map/all_to_all | solution.py:39
Sparse Core Ops, SparseCore 0:
  111.6 42.6 all-reduce.6
where the time goes:
time: 399 us; the launch traced here: 394 us
  blocking collectives  150 us (38%)
  other arithmetic  125 us (31%)
  waiting for transfers between devices  34.9 us (9%)
  local copies, waits for them, and re-layouts  33.3 us (8%)
  matrix products  19.1 us (5%)
  between operations  18.6 us (5%)
  starting transfers between devices  13.2 us (3%)
    another operation x14, other arithmetic, mixing_matrix(): factor = jnp.linalg.cholesky(system)  79 us
    another operation x3, other arithmetic, mixing_matrix(): solved = jax.scipy.linalg.cho_solve((factor, True), right_side)  40.3 us
    all_gather x1, blocking collectives, local(): obs_rows = lax.all_gather(local_rows, 'member', axis=0, tiled=True)  30.5 us
    all_to_all x1, blocking collectives, local(): lax.all_to_all(updated, 'member', split_axis=0, concat_axis=1, tiled=True)  29.1 us
    all_gather x1, blocking collectives, local(): region_offsets = lax.all_gather(obs_offset, 'member', axis=1, tiled=True)  22.5 us
    psum x1, blocking collectives, local(): products, column = lax.psum((products, column), 'region')  22.4 us
    all_to_all x1, waiting for transfers between devices, local(): lax.all_to_all(lax.all_to_all(ensemble, 'region', split_axis=1, concat_ax...  20.2 us
    all_gather x1, blocking collectives, local(): lax.all_gather(variance, 'member', axis=0, tiled=True)  17.1 us
  transfers between devices with their start and end apart: 4, of which 2 were waited for; matrix products, arithmetic and copies ran while one was open for 38% of the time, Pallas kernels for 0%

commit v1 on v0

--- a/solution.py
+++ b/solution.py
@@ -53,7 +53,14 @@
     own_rows = jnp.take(ensemble, link_index, axis=1).reshape(own_count, regions, -1)
     local_rows = lax.all_to_all(own_rows, "region", split_axis=1, concat_axis=0, tiled=True)
     local_rows = local_rows.reshape(own_count * regions, -1)
-    obs_rows = lax.all_gather(local_rows, "member", axis=0, tiled=True)
+    ring = [local_rows]
+    for hop in range(7):
+        ring.append(lax.ppermute(ring[-1], "member", [(dev, (dev + 1) % 8) for dev in range(8)]))
+    obs_rows = jnp.roll(
+        jnp.concatenate(ring[::-1], axis=0),
+        (lax.axis_index("member") + 1) * ring[0].shape[0],
+        axis=0,
+    )
     region_values, region_variance = (
         lax.all_gather(values, "member", axis=0, tiled=True),
         lax.all_gather(variance, "member", axis=0, tiled=True),

time: 399 us -> 410 us (1.028)
  waiting for transfers between devices: 34.9 us -> 70.9 us
  blocking collectives: 150 us -> 128 us
    ppermute x0 -> x7, waiting for transfers between devices: none -> 37.3 us  [local(): lax.ppermute(ring[-1], 'member', [(dev, (dev + 1) % 8) for dev in range(8)])]
    all_gather x1 -> x0, blocking collectives: 30.5 us -> none  [local(): obs_rows = lax.all_gather(local_rows, 'member', axis=0, tiled=True)]
    all_to_all x0 -> x1, blocking collectives: none -> 6.42 us  [local(): lax.all_to_all(own_rows, 'region', split_axis=1, concat_axis=0, tiled=True)]
    all_gather x1, blocking collectives: 17.1 us -> 21.8 us  [local(): lax.all_gather(variance, 'member', axis=0, tiled=True)]
    unnamed x19 -> x34, local copies, waits for them, and re-layouts: 9.77 us -> 9.83 us
  transfers between devices with their start and end apart: 4 -> 10, of which waited for: 2 -> 8; matrix products, arithmetic and copies ran while one was open for 38% -> 37% of each run, Pallas kernels for 0% -> 0%
where the time goes in v1:
time: 410 us; the launch traced here: 405 us
  blocking collectives  128 us (31%)
  other arithmetic  124 us (30%)
  waiting for transfers between devices  70.9 us (17%)
  local copies, waits for them, and re-layouts  33.4 us (8%)
  matrix products  19.1 us (5%)
  between operations  18.6 us (5%)
  starting transfers between devices  9.97 us (2%)
    another operation x14, other arithmetic, mixing_matrix(): factor = jnp.linalg.cholesky(system)  79 us
    another operation x3, other arithmetic, mixing_matrix(): solved = jax.scipy.linalg.cho_solve((factor, True), right_side)  40.3 us
    ppermute x7, waiting for transfers between devices, local(): lax.ppermute(ring[-1], 'member', [(dev, (dev + 1) % 8) for dev in range(8)])  37.3 us
    all_to_all x1, blocking collectives, local(): lax.all_to_all(updated, 'member', split_axis=0, concat_axis=1, tiled=True)  29.1 us
    all_gather x1, blocking collectives, local(): region_offsets = lax.all_gather(obs_offset, 'member', axis=1, tiled=True)  22.5 us
    all_gather x1, blocking collectives, local(): lax.all_gather(variance, 'member', axis=0, tiled=True)  21.8 us
    all_to_all x1, waiting for transfers between devices, local(): lax.all_to_all(lax.all_to_all(ensemble, 'region', split_axis=1, concat_ax...  20.2 us
    psum x1, blocking collectives, local(): products, column = lax.psum((products, column), 'region')  20.1 us
  transfers between devices with their start and end apart: 10, of which 8 were waited for; matrix products, arithmetic and copies ran while one was open for 37% of the time, Pallas kernels for 0%

profile of v1, /device:TPU:0, one launch (start us, length us, event | category | flops | bytes accessed | tf_op | source)
XLA Modules:
  0.0 404.7 jit_solution(14795665674492368618)
XLA Ops:
  6.5 22.5 %all_gather.13 = s32[1,8,16]{2,0,1:T(1,128)S(1)} all-gather(s32[1,1,16]{2,0,1:T(1,128)} %bitcast.114), channel_id=1, replica_groups=mesh['member'=8,'region'=4] {'member'}, dimensions={1}, use_global_device_ids=true | all-gather | bytes 576 | tf_op jit(solution)/shard_map/all_gather | solution.py:48
  34.5 7.1 %copy.51 = bf16[16,32768]{0,1:T(8,128)(2,1)} copy(bf16[16,32768]{1,0:T(8,128)(2,1)} %param.4) | data formatting | bytes 2097152 | tf_op args[0]
  47.3 6.4 %all_to_all.79 = bf16[16,4,128]{2,0,1:T(8,128)(2,1)S(1)} all-to-all(bf16[16,4,128]{2,0,1:T(8,128)(2,1)S(1)} %broadcast_select_fusion), channel_id=1, replica_groups=mesh['member'=8,'region'=4] {'region'}, dimensions={1} | all-to-all | bytes 32768 | tf_op jit(solution)/shard_map/all_to_all | solution.py:54
  53.7 6.4 %collective-permute-done = bf16[64,128]{1,0:T(8,128)(2,1)S(1)} collective-permute-done((bf16[64,128]{1,0:T(8,128)(2,1)S(1)}, bf16[64,128]{1,0:T(8,128)(2,1)S(1)}, u32[]{:S(2)}, u32[]{:S(2)}) %collective-permute-start) | collective-permute-done | bytes 16416 | tf_op jit(solution)/shard_map/ppermute | solution.py:58
  60.1 6.4 %collective-permute-done.1 = bf16[64,128]{1,0:T(8,128)(2,1)S(1)} collective-permute-done((bf16[64,128]{1,0:T(8,128)(2,1)S(1)}, bf16[64,128]{1,0:T(8,128)(2,1)S(1)}, u32[]{:S(2)}, u32[]{:S(2)}) %collective-permute-start.1) | collective-permute-done | bytes 16416 | tf_op jit(solution)/shard_map/ppermute | solution.py:58
  66.6 6.4 %collective-permute-done.2 = bf16[64,128]{1,0:T(8,128)(2,1)S(1)} collective-permute-done((bf16[64,128]{1,0:T(8,128)(2,1)S(1)}, bf16[64,128]{1,0:T(8,128)(2,1)S(1)}, u32[]{:S(2)}, u32[]{:S(2)}) %collective-permute-start.2) | collective-permute-done | bytes 16416 | tf_op jit(solution)/shard_map/ppermute | solution.py:58
  73.0 6.4 %collective-permute-done.3 = bf16[64,128]{1,0:T(8,128)(2,1)S(1)} collective-permute-done((bf16[64,128]{1,0:T(8,128)(2,1)S(1)}, bf16[64,128]{1,0:T(8,128)(2,1)S(1)}, u32[]{:S(2)}, u32[]{:S(2)}) %collective-permute-start.3) | collective-permute-done | bytes 16416 | tf_op jit(solution)/shard_map/ppermute | solution.py:58
  86.0 6.3 %collective-permute-done.5 = bf16[64,128]{1,0:T(8,128)(2,1)S(1)} collective-permute-done((bf16[64,128]{1,0:T(8,128)(2,1)S(1)}, bf16[64,128]{1,0:T(8,128)(2,1)S(1)}, u32[]{:S(2)}, u32[]{:S(2)}) %collective-permute-start.5) | collective-permute-done | bytes 16416 | tf_op jit(solution)/shard_map/ppermute | solution.py:58
  92.4 21.8 %all-reduce.3 = (f32[128]{0:T(128)S(1)}, f32[128]{0:T(128)S(1)}) all-reduce(f32[128]{0:T(128)S(1)} %bitcast_dynamic-update-slice_fusion.1, f32[128]{0:T(128)S(1)} %bitcast_dynamic-update-slice_fusion.2), channel_id=3, replica_groups=mesh['member'=8,'region'=4] {'member'}, use_global_device_ids=true, to_apply=%add.2 | all-reduce | flops 256 | bytes 2048 | tf_op jit(solution)/shard_map/all_gather | solution.py:66
  115.9 6.4 %all-reduce.4 = (f32[]{:T(128)}, f32[]{:T(128)}) all-reduce(f32[]{:T(128)} %get-tuple-element.54, f32[]{:T(128)} %get-tuple-element.51), channel_id=1, replica_groups=mesh['member'=8,'region'=4] {'region'}, use_global_device_ids=true, to_apply=%region_3.4 | all-reduce | flops 2 | bytes 16 | tf_op jit(solution)/shard_map/psum | solution.py:72
  131.2 20.1 %psum.31 = f32[512,1]{0,1:T(1,128)S(1)} all-reduce(f32[512,1]{0,1:T(1,128)S(1)} %convolution_bitcast_fusion), channel_id=1, replica_groups=mesh['member'=8,'region'=4] {'region'}, use_global_device_ids=true, to_apply=%region_16.17 | all-reduce | flops 512 | bytes 4096 | tf_op jit(solution)/shard_map/psum | solution.py:75
  151.4 13.5 %all-reduce.7.cloned.1.call-done = f32[512,512]{0,1:T(8,128)} async-done(((f32[512,512]{0,1:T(8,128)}), f32[512,512]{0,1:T(8,128)}) %all-reduce.7.cloned.1.call-update) | async-done | bytes 1048592 | tf_op jit(solution)/shard_map/psum | solution.py:75
  169.3 11.7 %cholesky.103 = f32[128,128]{1,0:T(8,128)S(1)} custom-call(f32[128,128]{1,0:T(8,128)S(1)} %cholesky.263), custom_call_target="Cholesky" | custom-call | tf_op jit(solution)/shard_map/jit(cholesky)/cholesky | solution.py:27
  181.0 9.8 %custom-call.34 = f32[1,128,128]{1,2,0:T(8,128)S(1)} custom-call(f32[1,128,128]{2,1,0:T(8,128)S(1)} %get-tuple-element.50), custom_call_target="InvertDiagBlocksLowerTriangular" | custom-call | tf_op jit(solution)/shard_map/jit(cholesky)/cholesky | solution.py:27
  191.5 11.7 %cholesky.215 = f32[128,128]{1,0:T(8,128)S(1)} custom-call(f32[128,128]{1,0:T(8,128)S(1)} %cholesky.267), custom_call_target="Cholesky" | custom-call | tf_op jit(solution)/shard_map/jit(cholesky)/cholesky | solution.py:27
  203.6 10.0 %custom-call.35 = f32[1,128,128]{1,2,0:T(8,128)S(1)} custom-call(f32[1,128,128]{2,1,0:T(8,128)S(1)} %get-tuple-element.48), custom_call_target="InvertDiagBlocksLowerTriangular" | custom-call | tf_op jit(solution)/shard_map/jit(cholesky)/cholesky | solution.py:27
  215.6 11.7 %cholesky.236 = f32[128,128]{1,0:T(8,128)S(1)} custom-call(f32[128,128]{1,0:T(8,128)S(1)} %cholesky.272), custom_call_target="Cholesky" | custom-call | tf_op jit(solution)/shard_map/jit(cholesky)/cholesky | solution.py:27
  227.5 9.8 %custom-call.36 = f32[1,128,128]{1,2,0:T(8,128)S(1)} custom-call(f32[1,128,128]{2,1,0:T(8,128)S(1)} %get-tuple-element.46), custom_call_target="InvertDiagBlocksLowerTriangular" | custom-call | tf_op jit(solution)/shard_map/jit(cholesky)/cholesky | solution.py:27
  238.9 12.1 %cholesky.253 = f32[128,128]{1,0:T(8,128)S(1)} custom-call(f32[128,128]{1,0:T(8,128)S(1)} %convolution_subtract_fusion.8), custom_call_target="Cholesky" | custom-call | tf_op jit(solution)/shard_map/jit(cholesky)/cholesky | solution.py:27
  255.9 11.0 %while.1 = (s32[]{:T(128)}, f32[512,512]{0,1:T(8,128)S(1)}, s32[4,2]{0,1:T(2,128)S(1)}, f32[4,128,128]{2,1,0:T(8,128)}, s32[]{:T(128)}) while((s32[]{:T(128)}, f32[512,512]{0,1:T(8,128)S(1)}, s32[4,2]{0,1:T(2,128)S(1)}, f32[4,128,128]{2,1,0:T(8,128)}, s32[]{:T(128)}) %tuple.30), condition=%wide.while_cond, body=%wide.while_body.sunk | while | flops 2 | bytes 393829 | solution.py:29
  266.8 40.1 %custom-call.37 = f32[4,128,128]{1,2,0:T(8,128)S(1)} custom-call(f32[4,128,128]{2,1,0:T(8,128)} %get-tuple-element.12), custom_call_target="InvertDiagBlocksLowerTriangular" | custom-call | tf_op jit(solution)/shard_map/jit(_cho_solve)/triangular_solve | solution.py:29
  325.2 20.2 %all-to-all-done.1 = bf16[64,8,1024]{2,0,1:T(8,128)(2,1)S(1)} async-done(((bf16[64,8,1024]{2,0,1:T(8,128)(2,1)}), bf16[64,8,1024]{2,0,1:T(8,128)(2,1)S(1)}, u32[]{:S(2)}, u32[]{:S(2)}) %all-to-all-start.1) | async-done | bytes 1048608 | tf_op jit(solution)/shard_map/all_to_all | solution.py:39
  349.6 29.1 %all_to_all.80 = bf16[8,64,1024]{2,1,0:T(8,128)(2,1)S(1)} all-to-all(bf16[8,64,1024]{2,1,0:T(8,128)(2,1)S(1)} %bitcast.106), channel_id=1, replica_groups=mesh['member'=8,'region'=4] {'member'}, dimensions={0} | all-to-all | bytes 2097152 | tf_op jit(solution)/shard_map/all_to_all | solution.py:83
  379.8 16.9 %all_to_all.81 = bf16[4,16,8192]{2,1,0:T(8,128)(2,1)S(1)} all-to-all(bf16[4,16,8192]{2,1,0:T(8,128)(2,1)S(1)} %all_to_all.70), channel_id=1, replica_groups=mesh['member'=8,'region'=4] {'region'}, dimensions={0} | all-to-all | bytes 2097152 | tf_op jit(solution)/shard_map/all_to_all | solution.py:82
  (143 shorter events, 73.2 us)
Async XLA Ops:
  6.5 158.3 %all-reduce.7.cloned.1.call-start = ((), (), s32[]{:S(2)}) async-start(), calls=%async_computation.5 | async-start | bytes 2097152 | tf_op jit(solution)/shard_map/psum | solution.py:75
  34.4 45.0 %copy-start.5 = (u32[32]{0:T(128)S(1)}, u32[32]{0:T(128)}, u32[]{:S(2)}) copy-start(u32[32]{0:T(128)} %constant.241) | copy-start | bytes 388
  34.5 51.4 %copy-start.3 = (f32[1,1,16]{2,1,0:T(1,128)S(1)}, f32[1,1,16]{2,1,0:T(1,128)}, u32[]{:S(2)}) copy-start(f32[1,1,16]{2,1,0:T(1,128)} %param.7) | copy-start | bytes 196
  34.5 57.8 %copy-start.4 = (f32[1,1,16]{2,1,0:T(1,128)S(1)}, f32[1,1,16]{2,1,0:T(1,128)}, u32[]{:S(2)}) copy-start(f32[1,1,16]{2,1,0:T(1,128)} %param.6) | copy-start | bytes 196
  41.5 84.1 %copy-start.1 = (bf16[16,32768]{1,0:T(8,128)(2,1)S(1)}, bf16[16,32768]{1,0:T(8,128)(2,1)}, u32[]{:S(2)}) copy-start(bf16[16,32768]{1,0:T(8,128)(2,1)} %param.4) | copy-start | bytes 3145732
  53.7 6.4 %collective-permute-start = (bf16[64,128]{1,0:T(8,128)(2,1)S(1)}, bf16[64,128]{1,0:T(8,128)(2,1)S(1)}, u32[]{:S(2)}, u32[]{:S(2)}) collective-permute-start(bf16[64,128]{1,0:T(8,128)(2,1)S(1)} %bitcast.108), channel_id=1, source_target_pairs={{0,4},{4,8},{8,12},{12,16},{16,20},{20,24},{24,28},{28,0},{1,5},{5... | collective-permute-start | bytes 49160 | tf_op jit(solution)/shard_map/ppermute | solution.py:58
  60.1 6.4 %collective-permute-start.1 = (bf16[64,128]{1,0:T(8,128)(2,1)S(1)}, bf16[64,128]{1,0:T(8,128)(2,1)S(1)}, u32[]{:S(2)}, u32[]{:S(2)}) collective-permute-start(bf16[64,128]{1,0:T(8,128)(2,1)S(1)} %collective-permute-done), channel_id=1, source_target_pairs={{0,4},{4,8},{8,12},{12,16},{16,20},{20,24},{24,28},{28,0},{1,5},{5... | collective-permute-start | bytes 49160 | tf_op jit(solution)/shard_map/ppermute | solution.py:58
  66.6 6.4 %collective-permute-start.2 = (bf16[64,128]{1,0:T(8,128)(2,1)S(1)}, bf16[64,128]{1,0:T(8,128)(2,1)S(1)}, u32[]{:S(2)}, u32[]{:S(2)}) collective-permute-start(bf16[64,128]{1,0:T(8,128)(2,1)S(1)} %collective-permute-done.1), channel_id=1, source_target_pairs={{0,4},{4,8},{8,12},{12,16},{16,20},{20,24},{24,28},{28,0},{1,5},{5... | collective-permute-start | bytes 49160 | tf_op jit(solution)/shard_map/ppermute | solution.py:58
  73.0 6.4 %collective-permute-start.3 = (bf16[64,128]{1,0:T(8,128)(2,1)S(1)}, bf16[64,128]{1,0:T(8,128)(2,1)S(1)}, u32[]{:S(2)}, u32[]{:S(2)}) collective-permute-start(bf16[64,128]{1,0:T(8,128)(2,1)S(1)} %collective-permute-done.2), channel_id=1, source_target_pairs={{0,4},{4,8},{8,12},{12,16},{16,20},{20,24},{24,28},{28,0},{1,5},{5... | collective-permute-start | bytes 49160 | tf_op jit(solution)/shard_map/ppermute | solution.py:58
  79.4 6.4 %collective-permute-start.4 = (bf16[64,128]{1,0:T(8,128)(2,1)S(1)}, bf16[64,128]{1,0:T(8,128)(2,1)S(1)}, u32[]{:S(2)}, u32[]{:S(2)}) collective-permute-start(bf16[64,128]{1,0:T(8,128)(2,1)S(1)} %collective-permute-done.3), channel_id=1, source_target_pairs={{0,4},{4,8},{8,12},{12,16},{16,20},{20,24},{24,28},{28,0},{1,5},{5... | collective-permute-start | bytes 49160 | tf_op jit(solution)/shard_map/ppermute | solution.py:58
  85.9 6.4 %collective-permute-start.5 = (bf16[64,128]{1,0:T(8,128)(2,1)S(1)}, bf16[64,128]{1,0:T(8,128)(2,1)S(1)}, u32[]{:S(2)}, u32[]{:S(2)}) collective-permute-start(bf16[64,128]{1,0:T(8,128)(2,1)S(1)} %collective-permute-done.4), channel_id=1, source_target_pairs={{0,4},{4,8},{8,12},{12,16},{16,20},{20,24},{24,28},{28,0},{1,5},{5... | collective-permute-start | bytes 49160 | tf_op jit(solution)/shard_map/ppermute | solution.py:58
  92.3 21.9 %collective-permute-start.6 = (bf16[64,128]{1,0:T(8,128)(2,1)S(1)}, bf16[64,128]{1,0:T(8,128)(2,1)S(1)}, u32[]{:S(2)}, u32[]{:S(2)}) collective-permute-start(bf16[64,128]{1,0:T(8,128)(2,1)S(1)} %collective-permute-done.5), channel_id=1, source_target_pairs={{0,4},{4,8},{8,12},{12,16},{16,20},{20,24},{24,28},{28,0},{1,5},{5... | collective-permute-start | bytes 49160 | tf_op jit(solution)/shard_map/ppermute | solution.py:58
  126.6 184.3 %all-to-all-start = ((bf16[16,4,8192]{2,0,1:T(8,128)(2,1)}), bf16[16,4,8192]{2,0,1:T(8,128)(2,1)}, u32[]{:S(2)}, u32[]{:S(2)}) async-start(bf16[16,4,8192]{2,0,1:T(8,128)(2,1)} %bitcast.95), calls=%async_computation | async-start | bytes 2097152 | tf_op jit(solution)/shard_map/all_to_all | solution.py:40
  164.8 2.9 copy-start
  169.2 34.3 %copy-start.2 = (f32[512,512]{1,0:T(8,128)}, f32[512,512]{1,0:T(8,128)S(1)}, u32[]{:S(2)}) copy-start(f32[512,512]{1,0:T(8,128)S(1)} %fusion.4) | copy-start | bytes 3145732
  314.3 31.1 %all-to-all-start.1 = ((bf16[64,8,1024]{2,0,1:T(8,128)(2,1)}), bf16[64,8,1024]{2,0,1:T(8,128)(2,1)S(1)}, u32[]{:S(2)}, u32[]{:S(2)}) async-start(bf16[64,8,1024]{2,0,1:T(8,128)(2,1)} %copy.48), calls=%async_computation.1 | async-start | bytes 2097152 | tf_op jit(solution)/shard_map/all_to_all | solution.py:39
Sparse Core Ops, SparseCore 0:
  125.7 39.0 all-reduce.6
